TPU v7x, 256 devices: a whole 4x4x8 slice. The times are simulated.
256 devices in a mesh: blk: 16 (over x, z_hi), slab: 16 (over y, z_lo, core).
Axes of the slice: x: 4, y: 4, z: 8 (z_hi: 4, z_lo: 2; z = z_hi * 2 + z_lo), core: 2. Of those that a mesh axis runs over, the one named last changes fastest.
Arguments:
- xinv: bfloat16 [16, 4096, 4096], P('blk', None, 'slab'), may hold values from -1 to 16
- ymat: bfloat16 [16, 4096, 4096], P('blk', None, 'slab'), may hold values from -1 to 16
- basis: bfloat16 [16, 4096, 1024], P('blk', 'slab'), may hold values from -0.08118988 to 0.08118988
- pair_index: int32 [16, 2, 512], P('blk'), may hold values from 0 to 1023
- orders: int32 [16], replicated, may hold values from 1 to 512, 4096 in all
- dest: int32 [16], replicated, may hold values from 0 to 15, each once
Outputs:
- factor: float32 [16, 512, 512], P('blk', 'slab')
Inputs may be any that keep to these rules, and one draw needn't show every extreme that they name: `pair_index`: entries name columns of the block's basis. Sum of all orders is 4096; the largest equals 512. `dest`: every group receives exactly one block.
All inputs are finite; a program needn't handle non-finite values.
Results may differ from a plain program's by a relative error of at most 0.0003.
Values may be sent and summed in bfloat16 or wider, within the bound.
A program may use at most 64 MiB of HBM per device.

v0:
```python
import jax
import jax.numpy as jnp
from jax import lax
from jax.sharding import PartitionSpec as P


def cut_along(value, dim, length):
    before, after = (value.shape[:dim], value.shape[dim + 1 :])
    return jnp.moveaxis(value.reshape(*before, length, -1, *after), dim, 0)


def sum_at_owner(value, axis, dim):
    parts = cut_along(value, dim, lax.axis_size(axis))
    arrived = lax.all_to_all(parts, axis, split_axis=0, concat_axis=0, tiled=True)
    return arrived.sum(axis=0)


def from_everyone(value, axis):
    copies = jnp.broadcast_to(value, (lax.axis_size(axis), *value.shape))
    return lax.all_to_all(copies, axis, split_axis=0, concat_axis=0, tiled=True)


def in_order(parts, dim):
    parts = jnp.moveaxis(parts, 0, dim)
    lengths = parts.shape
    return parts.reshape(*lengths[:dim], lengths[dim] * lengths[dim + 1], *lengths[dim + 2 :])


def gathered_copies(value, axis, dim):
    parts = from_everyone(value, axis)
    return in_order(parts, dim)


def add_piece(piece, columns):
    return lax.dot_general(
        piece, columns, (((0,), (0,)), ((), ())), preferred_element_type=jnp.float32
    )


def on_device(xinv, ymat, basis, pair_index, orders, dest):
    xlocal = xinv[0]
    ylocal = ymat[0]
    vlocal = basis[0]
    piece = lax.all_gather(vlocal, "slab", axis=0, tiled=True)
    cx = add_piece(piece, xlocal)
    cy = add_piece(piece, ylocal)
    cx = cx.astype(jnp.bfloat16)
    cy = cy.astype(jnp.bfloat16)
    first = pair_index[0, 0]
    second = pair_index[0, 1]
    order_most = first.shape[0]
    share = order_most // lax.axis_size("slab")
    row_start = lax.axis_index("slab") * share
    basis_first = jnp.take(vlocal, first, axis=1)
    basis_second = jnp.take(vlocal, second, axis=1)
    cx_first = jnp.take(cx, first, axis=0)
    cy_second = jnp.take(cy, second, axis=0)
    stacked = sum_at_owner(
        jnp.concatenate(
            [
                jnp.dot(cx_first, basis_first, preferred_element_type=jnp.float32),
                jnp.dot(cy_second, basis_second, preferred_element_type=jnp.float32),
            ],
            axis=1,
        ),
        "slab",
        0,
    )
    a_ff = stacked[:, :order_most]
    b_ss = stacked[:, order_most:]
    schur = a_ff * b_ss
    block_id = lax.axis_index("blk")
    order = orders[block_id]
    row_ids = row_start + jnp.arange(share, dtype=jnp.int32)
    col_ids = jnp.arange(order_most, dtype=jnp.int32)
    mask = (row_ids[:, None] < order) & (col_ids[None, :] < order)
    diagonal = (row_ids[:, None] == col_ids[None, :]).astype(jnp.float32)
    schur_rows = jnp.where(mask, schur, 0.0) + diagonal
    everyone = gathered_copies(schur_rows, "blk", 0)
    groups = dest.shape[0]
    everyone = everyone.reshape(groups, share, order_most)
    chosen = (dest == block_id).astype(jnp.float32)
    mine = jnp.sum(chosen[:, None, None] * everyone, axis=0)
    whole = gathered_copies(mine, "slab", 0)
    lower = jnp.linalg.cholesky(whole)
    own = lax.dynamic_slice_in_dim(lower, row_start, share, 0)
    return own[None]


def solution(mesh):
    return jax.shard_map(
        on_device,
        mesh=mesh,
        in_specs=(
            P("blk", None, "slab"),
            P("blk", None, "slab"),
            P("blk", "slab", None),
            P("blk", None, None),
            P(),
            P(),
        ),
        out_specs=P("blk", "slab", None),
        check_vma=False,
    )
```

profile of v0, /device:TPU:1, one launch (start us, length us, event | category | flops | bytes accessed | tf_op | source)
XLA Modules:
  0.0 283.8 jit_solution(7355366731148311306)
XLA Ops:
  7.3 1.2 copy.12
  9.3 2.0 gather_fusion.1
  11.3 2.0 gather_fusion.3
  13.3 54.8 %all-gather.3.cloned.1.call-done = bf16[1,4096,1024]{2,1,0:T(8,128)(2,1)} async-done(((bf16[1,256,1024]{2,1,0:T(8,128)(2,1)}), bf16[1,4096,1024]{2,1,0:T(8,128)(2,1)}) %all-gather.3.cloned.1.call-update) | async-done | bytes 8388624 | tf_op jit(solution)/shard_map/all_gather | solution.py:44
  68.1 5.8 %fusion.6 = bf16[1024,256]{1,0:T(8,128)(2,1)S(1)} fusion(bf16[1,4096,256]{2,1,0:T(8,128)(2,1)S(1)} %copy-done, bf16[1,4096,1024]{2,1,0:T(8,128)(2,1)} %all-gather.3.cloned.1.call-done), kind=kOutput, calls=%fused_computation.11 | convolution fusion | flops 2147745792 | bytes 11010048 | tf_op jit(solution)/shard_map/dot_general | solution.py:35
  73.8 2.0 gather_fusion
  75.8 6.3 %fusion.11 = bf16[1024,256]{1,0:T(8,128)(2,1)S(1)} fusion(bf16[1,4096,256]{2,1,0:T(8,128)(2,1)} %param.11, bf16[1,4096,1024]{2,1,0:T(8,128)(2,1)} %all-gather.3.cloned.1.call-done), kind=kOutput, calls=%fused_computation.12 | convolution fusion | flops 2147745792 | bytes 11010048 | tf_op jit(solution)/shard_map/dot_general | solution.py:35
  82.1 2.6 gather_fusion.2
  84.7 1.4 fusion.18
  86.5 1.5 pad_maximum_fusion
  88.0 2.9 %copy.13 = f32[512,1024]{1,0:T(8,128)} copy(f32[512,1024]{0,1:T(8,128)} %pad_maximum_fusion) | data formatting | bytes 4194304 | tf_op jit(solution)/shard_map/concatenate | solution.py:59
  90.9 5.3 %all-to-all-start = ((f32[16,32,1024]{2,1,0:T(8,128)}), f32[16,32,1024]{2,1,0:T(8,128)}, u32[]{:S(2)}, u32[]{:S(2)}) async-start(f32[16,32,1024]{2,1,0:T(8,128)} %bitcast.59), calls=%async_computation | async-start | bytes 4194304 | tf_op jit(solution)/shard_map/all_to_all | solution.py:14
  98.2 25.1 %all-to-all-done = f32[16,32,1024]{2,1,0:T(8,128)} async-done(((f32[16,32,1024]{2,1,0:T(8,128)}), f32[16,32,1024]{2,1,0:T(8,128)}, u32[]{:S(2)}, u32[]{:S(2)}) %all-to-all-start) | async-done | bytes 2097184 | tf_op jit(solution)/shard_map/all_to_all | solution.py:14
  123.3 1.7 reduce_sum.18
  125.1 1.1 broadcast_in_dim.39
  126.3 8.4 %all-to-all-start.1 = ((f32[16,32,512]{2,1,0:T(8,128)}), f32[16,32,512]{2,1,0:T(8,128)S(1)}, u32[]{:S(2)}, u32[]{:S(2)}) async-start(f32[16,32,512]{2,1,0:T(8,128)} %broadcast_in_dim.39), calls=%async_computation.1 | async-start | bytes 2097152 | tf_op jit(solution)/shard_map/all_to_all | solution.py:20
  134.7 24.1 %all-to-all-done.1 = f32[16,32,512]{2,1,0:T(8,128)S(1)} async-done(((f32[16,32,512]{2,1,0:T(8,128)}), f32[16,32,512]{2,1,0:T(8,128)S(1)}, u32[]{:S(2)}, u32[]{:S(2)}) %all-to-all-start.1) | async-done | bytes 1048608 | tf_op jit(solution)/shard_map/all_to_all | solution.py:20
  160.1 9.9 %all-to-all-start.2 = ((f32[16,32,512]{2,1,0:T(8,128)}), f32[16,32,512]{2,1,0:T(8,128)S(1)}, u32[]{:S(2)}, u32[]{:S(2)}) async-start(f32[16,32,512]{2,1,0:T(8,128)} %broadcast_in_dim.40), calls=%async_computation.2 | async-start | bytes 2097152 | tf_op jit(solution)/shard_map/all_to_all | solution.py:20
  170.0 15.7 %all-to-all-done.2 = f32[16,32,512]{2,1,0:T(8,128)S(1)} async-done(((f32[16,32,512]{2,1,0:T(8,128)}), f32[16,32,512]{2,1,0:T(8,128)S(1)}, u32[]{:S(2)}, u32[]{:S(2)}) %all-to-all-start.2) | async-done | bytes 1048608 | tf_op jit(solution)/shard_map/all_to_all | solution.py:20
  185.6 1.3 copy.14
  187.0 1.4 fusion.16
  189.3 11.7 %cholesky.104 = f32[128,128]{1,0:T(8,128)S(1)} custom-call(f32[128,128]{1,0:T(8,128)S(1)} %cholesky.266), custom_call_target="Cholesky" | custom-call | tf_op jit(solution)/shard_map/jit(cholesky)/cholesky | solution.py:85
  201.2 9.8 %custom-call.27 = f32[1,128,128]{1,2,0:T(8,128)S(1)} custom-call(f32[1,128,128]{2,1,0:T(8,128)S(1)} %get-tuple-element.16), custom_call_target="InvertDiagBlocksLowerTriangular" | custom-call | tf_op jit(solution)/shard_map/jit(cholesky)/cholesky | solution.py:85
  211.0 1.2 constant_dynamic-update-slice_fusion.2
  212.3 1.3 convolution_subtract_fusion
  213.6 11.7 %cholesky.217 = f32[128,128]{1,0:T(8,128)S(1)} custom-call(f32[128,128]{1,0:T(8,128)S(1)} %cholesky.270), custom_call_target="Cholesky" | custom-call | tf_op jit(solution)/shard_map/jit(cholesky)/cholesky | solution.py:85
  225.3 10.0 %custom-call.28 = f32[1,128,128]{1,2,0:T(8,128)S(1)} custom-call(f32[1,128,128]{2,1,0:T(8,128)S(1)} %get-tuple-element.13), custom_call_target="InvertDiagBlocksLowerTriangular" | custom-call | tf_op jit(solution)/shard_map/jit(cholesky)/cholesky | solution.py:85
  235.6 1.3 convolution_subtract_fusion.1
  236.9 11.7 %cholesky.238 = f32[128,128]{1,0:T(8,128)S(1)} custom-call(f32[128,128]{1,0:T(8,128)S(1)} %cholesky.275), custom_call_target="Cholesky" | custom-call | tf_op jit(solution)/shard_map/jit(cholesky)/cholesky | solution.py:85
  249.3 9.8 %custom-call.29 = f32[1,128,128]{1,2,0:T(8,128)S(1)} custom-call(f32[1,128,128]{2,1,0:T(8,128)S(1)} %get-tuple-element.10), custom_call_target="InvertDiagBlocksLowerTriangular" | custom-call | tf_op jit(solution)/shard_map/jit(cholesky)/cholesky | solution.py:85
  259.4 1.2 convolution_subtract_fusion.2
  260.6 11.7 %cholesky.255 = f32[128,128]{1,0:T(8,128)S(1)} custom-call(f32[128,128]{1,0:T(8,128)S(1)} %convolution_subtract_fusion.2), custom_call_target="Cholesky" | custom-call | tf_op jit(solution)/shard_map/jit(cholesky)/cholesky | solution.py:85
  (40 shorter events, 9.6 us)
Async XLA Ops:
  6.5 61.5 %copy-start = (bf16[1,4096,256]{2,1,0:T(8,128)(2,1)S(1)}, bf16[1,4096,256]{2,1,0:T(8,128)(2,1)}, u32[]{:S(2)}) copy-start(bf16[1,4096,256]{2,1,0:T(8,128)(2,1)} %param.10) | copy-start | bytes 6291460
  6.5 61.5 %all-gather.3.cloned.1.call-start = ((), (), s32[]{:S(2)}) async-start(), calls=%async_computation.3 | async-start | bytes 8912896 | tf_op jit(solution)/shard_map/all_gather | solution.py:44
  90.9 5.3 %copy-start.2 = (s32[16]{0:T(128)S(1)}, s32[16]{0:T(128)}, u32[]{:S(2)}) copy-start(s32[16]{0:T(128)} %param.14) | copy-start | bytes 196
  90.9 32.4 %all-to-all-start = ((f32[16,32,1024]{2,1,0:T(8,128)}), f32[16,32,1024]{2,1,0:T(8,128)}, u32[]{:S(2)}, u32[]{:S(2)}) async-start(f32[16,32,1024]{2,1,0:T(8,128)} %bitcast.59), calls=%async_computation | async-start | bytes 4194304 | tf_op jit(solution)/shard_map/all_to_all | solution.py:14
  125.0 9.7 %copy-start.3 = (s32[16]{0:T(128)S(1)}, s32[16]{0:T(128)}, u32[]{:S(2)}) copy-start(s32[16]{0:T(128)} %param.15) | copy-start | bytes 196
  126.3 32.5 %all-to-all-start.1 = ((f32[16,32,512]{2,1,0:T(8,128)}), f32[16,32,512]{2,1,0:T(8,128)S(1)}, u32[]{:S(2)}, u32[]{:S(2)}) async-start(f32[16,32,512]{2,1,0:T(8,128)} %broadcast_in_dim.39), calls=%async_computation.1 | async-start | bytes 2097152 | tf_op jit(solution)/shard_map/all_to_all | solution.py:20
  160.1 25.6 %all-to-all-start.2 = ((f32[16,32,512]{2,1,0:T(8,128)}), f32[16,32,512]{2,1,0:T(8,128)S(1)}, u32[]{:S(2)}, u32[]{:S(2)}) async-start(f32[16,32,512]{2,1,0:T(8,128)} %broadcast_in_dim.40), calls=%async_computation.2 | async-start | bytes 2097152 | tf_op jit(solution)/shard_map/all_to_all | solution.py:20
  188.3 1.0 copy-start.1
Sparse Core Ops, SparseCore 0:
  9.2 58.8 all-gather.2
where the time goes:
time: 284 us
  waiting for transfers between devices  120 us (42%)
  other arithmetic  85.4 us (30%)
  starting transfers between devices  23.7 us (8%)
  matrix products  19.3 us (7%)
  local copies, waits for them, and re-layouts  18.7 us (7%)
  between operations  16.3 us (6%)
    another operation x14, other arithmetic, on_device(): lower = jnp.linalg.cholesky(whole)  78.7 us
    all_gather x1, waiting for transfers between devices, on_device(): piece = lax.all_gather(vlocal, 'slab', axis=0, tiled=True)  54.8 us
    all_to_all x2, waiting for transfers between devices, from_everyone(): return lax.all_to_all(copies, axis, split_axis=0, concat_axis=0, tiled=True)  39.7 us
    all_to_all x1, waiting for transfers between devices, sum_at_owner(): lax.all_to_all(parts, axis, split_axis=0, concat_axis=0, tiled=True)  25.1 us
    all_to_all x2, starting transfers between devices, from_everyone(): return lax.all_to_all(copies, axis, split_axis=0, concat_axis=0, tiled=True)  18.4 us
    dot_general x2, matrix products, add_piece(): lax.dot_general(piece, columns, (((0,), (0,)), ((), ())), preferred_eleme...  12.1 us
  transfers between devices with their start and end apart: 4, of which 4 were waited for; matrix products, arithmetic and copies ran while one was open for 3% of the time, Pallas kernels for 0%

commit v1 on v0

--- a/solution.py
+++ b/solution.py
@@ -2,6 +2,7 @@
 import jax.numpy as jnp
 from jax import lax
 from jax.sharding import PartitionSpec as P
+from jax.lax import all_to_all, axis_size
 
 
 def cut_along(value, dim, length):
@@ -41,7 +42,9 @@
     xlocal = xinv[0]
     ylocal = ymat[0]
     vlocal = basis[0]
-    piece = lax.all_gather(vlocal, "slab", axis=0, tiled=True)
+    piece = jnp.concatenate(
+        all_to_all(jnp.stack([vlocal for _ in range(axis_size("slab"))]), "slab", 0, 0), axis=0
+    )
     cx = add_piece(piece, xlocal)
     cy = add_piece(piece, ylocal)
     cx = cx.astype(jnp.bfloat16)

time: 284 us -> 318 us (1.12)
  waiting for transfers between devices: 120 us -> 155 us
  between operations: 16.3 us -> 2.9 us
  starting transfers between devices: 23.7 us -> 32.4 us
  local copies, waits for them, and re-layouts: 18.7 us -> 22.4 us
    all_to_all x0 -> x1, waiting for transfers between devices: none -> 90.3 us  [on_device(): all_to_all(jnp.stack([vlocal for _ in range(axis_size('slab'))]), 'slab',...]
    all_gather x1 -> x0, waiting for transfers between devices: 54.8 us -> none  [on_device(): piece = lax.all_gather(vlocal, 'slab', axis=0, tiled=True)]
    all_to_all x0 -> x1, starting transfers between devices: none -> 7.8 us  [on_device(): all_to_all(jnp.stack([vlocal for _ in range(axis_size('slab'))]), 'slab',...]
    another operation x0 -> x1, local copies, waits for them, and re-layouts: none -> 5.48 us  [on_device(): jnp.stack([vlocal for _ in range(axis_size('slab'))])]
  transfers between devices with their start and end apart: 4 -> 4, of which waited for: 4 -> 4; matrix products, arithmetic and copies ran while one was open for 3% -> 2% of each run, Pallas kernels for 0% -> 0%
where the time goes in v1:
time: 318 us
  waiting for transfers between devices  155 us (49%)
  other arithmetic  85.4 us (27%)
  starting transfers between devices  32.4 us (10%)
  local copies, waits for them, and re-layouts  22.4 us (7%)
  matrix products  19.4 us (6%)
    all_to_all x1, waiting for transfers between devices, on_device(): all_to_all(jnp.stack([vlocal for _ in range(axis_size('slab'))]), 'slab',...  90.3 us
    another operation x14, other arithmetic, on_device(): lower = jnp.linalg.cholesky(whole)  78.7 us
    all_to_all x2, waiting for transfers between devices, from_everyone(): return lax.all_to_all(copies, axis, split_axis=0, concat_axis=0, tiled=True)  39.7 us
    all_to_all x1, waiting for transfers between devices, sum_at_owner(): lax.all_to_all(parts, axis, split_axis=0, concat_axis=0, tiled=True)  25.2 us
    all_to_all x2, starting transfers between devices, from_everyone(): return lax.all_to_all(copies, axis, split_axis=0, concat_axis=0, tiled=True)  19.3 us
    dot_general x2, matrix products, add_piece(): lax.dot_general(piece, columns, (((0,), (0,)), ((), ())), preferred_eleme...  12.1 us
    all_to_all x1, starting transfers between devices, on_device(): all_to_all(jnp.stack([vlocal for _ in range(axis_size('slab'))]), 'slab',...  7.8 us
  transfers between devices with their start and end apart: 4, of which 4 were waited for; matrix products, arithmetic and copies ran while one was open for 2% of the time, Pallas kernels for 0%

profile of v1, /device:TPU:1, one launch (start us, length us, event | category | flops | bytes accessed | tf_op | source)
XLA Modules:
  0.0 317.7 jit_solution(18185690546798684458)
XLA Ops:
  0.0 5.5 %stack.3 = bf16[16,256,1024]{2,1,0:T(8,128)(2,1)} broadcast(bf16[256,1024]{1,0:T(8,128)(2,1)} %bitcast.55), dimensions={1,2} | broadcast | bytes 8912896 | tf_op jit(solution)/shard_map/stack | solution.py:46
  5.5 7.8 %all-to-all-start = ((bf16[16,256,1024]{2,1,0:T(8,128)(2,1)}), bf16[16,256,1024]{2,1,0:T(8,128)(2,1)}, u32[]{:S(2)}, u32[]{:S(2)}) async-start(bf16[16,256,1024]{2,1,0:T(8,128)(2,1)} %stack.3), calls=%async_computation | async-start | bytes 16777216 | tf_op jit(solution)/shard_map/all_to_all | solution.py:46
  13.5 2.0 gather_fusion.1
  15.5 2.0 gather_fusion.3
  17.5 90.3 %all-to-all-done = bf16[16,256,1024]{2,1,0:T(8,128)(2,1)} async-done(((bf16[16,256,1024]{2,1,0:T(8,128)(2,1)}), bf16[16,256,1024]{2,1,0:T(8,128)(2,1)}, u32[]{:S(2)}, u32[]{:S(2)}) %all-to-all-start) | async-done | bytes 8388640 | tf_op jit(solution)/shard_map/all_to_all | solution.py:46
  107.8 5.8 %fusion.4 = bf16[1024,256]{1,0:T(8,128)(2,1)S(1)} fusion(bf16[4096,1024]{1,0:T(8,128)(2,1)} %bitcast.4, bf16[1,4096,256]{2,1,0:T(8,128)(2,1)S(1)} %copy-done), kind=kOutput, calls=%fused_computation.9 | convolution fusion | flops 2147745792 | bytes 11010048 | tf_op jit(solution)/shard_map/dot_general | solution.py:36
  113.6 2.0 gather_fusion
  115.6 6.4 %fusion.7 = bf16[1024,256]{1,0:T(8,128)(2,1)S(1)} fusion(bf16[4096,1024]{1,0:T(8,128)(2,1)} %bitcast.4, bf16[1,4096,256]{2,1,0:T(8,128)(2,1)} %param.11), kind=kOutput, calls=%fused_computation.10 | convolution fusion | flops 2147745792 | bytes 11010048 | tf_op jit(solution)/shard_map/dot_general | solution.py:36
  121.9 2.6 gather_fusion.2
  124.9 1.4 fusion.12
  126.3 1.5 pad_maximum_fusion
  127.8 2.9 copy.16
  130.7 5.3 %all-to-all-start.1 = ((f32[16,32,1024]{2,1,0:T(8,128)}), f32[16,32,1024]{2,1,0:T(8,128)}, u32[]{:S(2)}, u32[]{:S(2)}) async-start(f32[16,32,1024]{2,1,0:T(8,128)} %bitcast.54), calls=%async_computation.1 | async-start | bytes 4194304 | tf_op jit(solution)/shard_map/all_to_all | solution.py:15
  137.9 25.2 %all-to-all-done.1 = f32[16,32,1024]{2,1,0:T(8,128)} async-done(((f32[16,32,1024]{2,1,0:T(8,128)}), f32[16,32,1024]{2,1,0:T(8,128)}, u32[]{:S(2)}, u32[]{:S(2)}) %all-to-all-start.1) | async-done | bytes 2097184 | tf_op jit(solution)/shard_map/all_to_all | solution.py:15
  163.1 1.7 reduce_sum.18
  166.1 9.4 %all-to-all-start.2 = ((f32[16,32,512]{2,1,0:T(8,128)}), f32[16,32,512]{2,1,0:T(8,128)S(1)}, u32[]{:S(2)}, u32[]{:S(2)}) async-start(f32[16,32,512]{2,1,0:T(8,128)} %broadcast_in_dim.39), calls=%async_computation.2 | async-start | bytes 2097152 | tf_op jit(solution)/shard_map/all_to_all | solution.py:21
  175.5 24.1 %all-to-all-done.2 = f32[16,32,512]{2,1,0:T(8,128)S(1)} async-done(((f32[16,32,512]{2,1,0:T(8,128)}), f32[16,32,512]{2,1,0:T(8,128)S(1)}, u32[]{:S(2)}, u32[]{:S(2)}) %all-to-all-start.2) | async-done | bytes 1048608 | tf_op jit(solution)/shard_map/all_to_all | solution.py:21
  200.8 9.9 %all-to-all-start.3 = ((f32[16,32,512]{2,1,0:T(8,128)}), f32[16,32,512]{2,1,0:T(8,128)S(1)}, u32[]{:S(2)}, u32[]{:S(2)}) async-start(f32[16,32,512]{2,1,0:T(8,128)} %broadcast_in_dim.40), calls=%async_computation.3 | async-start | bytes 2097152 | tf_op jit(solution)/shard_map/all_to_all | solution.py:21
  210.8 15.7 %all-to-all-done.3 = f32[16,32,512]{2,1,0:T(8,128)S(1)} async-done(((f32[16,32,512]{2,1,0:T(8,128)}), f32[16,32,512]{2,1,0:T(8,128)S(1)}, u32[]{:S(2)}, u32[]{:S(2)}) %all-to-all-start.3) | async-done | bytes 1048608 | tf_op jit(solution)/shard_map/all_to_all | solution.py:21
  226.4 1.3 copy.17
  227.8 1.4 fusion.10
  230.1 11.7 %cholesky.104 = f32[128,128]{1,0:T(8,128)S(1)} custom-call(f32[128,128]{1,0:T(8,128)S(1)} %cholesky.266), custom_call_target="Cholesky" | custom-call | tf_op jit(solution)/shard_map/jit(cholesky)/cholesky | solution.py:88
  242.0 9.8 %custom-call.27 = f32[1,128,128]{1,2,0:T(8,128)S(1)} custom-call(f32[1,128,128]{2,1,0:T(8,128)S(1)} %get-tuple-element.16), custom_call_target="InvertDiagBlocksLowerTriangular" | custom-call | tf_op jit(solution)/shard_map/jit(cholesky)/cholesky | solution.py:88
  251.8 1.2 constant_dynamic-update-slice_fusion.2
  253.1 1.3 convolution_subtract_fusion
  254.3 11.7 %cholesky.217 = f32[128,128]{1,0:T(8,128)S(1)} custom-call(f32[128,128]{1,0:T(8,128)S(1)} %cholesky.270), custom_call_target="Cholesky" | custom-call | tf_op jit(solution)/shard_map/jit(cholesky)/cholesky | solution.py:88
  266.1 10.0 %custom-call.28 = f32[1,128,128]{1,2,0:T(8,128)S(1)} custom-call(f32[1,128,128]{2,1,0:T(8,128)S(1)} %get-tuple-element.13), custom_call_target="InvertDiagBlocksLowerTriangular" | custom-call | tf_op jit(solution)/shard_map/jit(cholesky)/cholesky | solution.py:88
  276.4 1.3 convolution_subtract_fusion.1
  277.7 11.7 %cholesky.238 = f32[128,128]{1,0:T(8,128)S(1)} custom-call(f32[128,128]{1,0:T(8,128)S(1)} %cholesky.275), custom_call_target="Cholesky" | custom-call | tf_op jit(solution)/shard_map/jit(cholesky)/cholesky | solution.py:88
  290.1 9.8 %custom-call.29 = f32[1,128,128]{1,2,0:T(8,128)S(1)} custom-call(f32[1,128,128]{2,1,0:T(8,128)S(1)} %get-tuple-element.10), custom_call_target="InvertDiagBlocksLowerTriangular" | custom-call | tf_op jit(solution)/shard_map/jit(cholesky)/cholesky | solution.py:88
  300.2 1.2 convolution_subtract_fusion.2
  301.4 11.7 %cholesky.255 = f32[128,128]{1,0:T(8,128)S(1)} custom-call(f32[128,128]{1,0:T(8,128)S(1)} %convolution_subtract_fusion.2), custom_call_target="Cholesky" | custom-call | tf_op jit(solution)/shard_map/jit(cholesky)/cholesky | solution.py:88
  (44 shorter events, 9.5 us)
Async XLA Ops:
  0.0 107.8 %copy-start = (bf16[1,4096,256]{2,1,0:T(8,128)(2,1)S(1)}, bf16[1,4096,256]{2,1,0:T(8,128)(2,1)}, u32[]{:S(2)}) copy-start(bf16[1,4096,256]{2,1,0:T(8,128)(2,1)} %param.10) | copy-start | bytes 6291460
  5.5 7.8 %copy-start.2 = (bf16[1,256,1024]{2,1,0:T(8,128)(2,1)S(1)}, bf16[1,256,1024]{2,1,0:T(8,128)(2,1)}, u32[]{:S(2)}) copy-start(bf16[1,256,1024]{2,1,0:T(8,128)(2,1)} %param.12) | copy-start | bytes 1572868
  5.5 8.0 %copy-start.3 = (s32[1,2,512]{2,1,0:T(2,128)S(1)}, s32[1,2,512]{2,1,0:T(2,128)}, u32[]{:S(2)}) copy-start(s32[1,2,512]{2,1,0:T(2,128)} %param.13) | copy-start | bytes 12292
  5.5 102.4 %all-to-all-start = ((bf16[16,256,1024]{2,1,0:T(8,128)(2,1)}), bf16[16,256,1024]{2,1,0:T(8,128)(2,1)}, u32[]{:S(2)}, u32[]{:S(2)}) async-start(bf16[16,256,1024]{2,1,0:T(8,128)(2,1)} %stack.3), calls=%async_computation | async-start | bytes 16777216 | tf_op jit(solution)/shard_map/all_to_all | solution.py:46
  130.7 5.3 %copy-start.4 = (s32[16]{0:T(128)S(1)}, s32[16]{0:T(128)}, u32[]{:S(2)}) copy-start(s32[16]{0:T(128)} %param.14) | copy-start | bytes 196
  130.7 32.4 %all-to-all-start.1 = ((f32[16,32,1024]{2,1,0:T(8,128)}), f32[16,32,1024]{2,1,0:T(8,128)}, u32[]{:S(2)}, u32[]{:S(2)}) async-start(f32[16,32,1024]{2,1,0:T(8,128)} %bitcast.54), calls=%async_computation.1 | async-start | bytes 4194304 | tf_op jit(solution)/shard_map/all_to_all | solution.py:15
  164.8 10.7 %copy-start.5 = (s32[16]{0:T(128)S(1)}, s32[16]{0:T(128)}, u32[]{:S(2)}) copy-start(s32[16]{0:T(128)} %param.15) | copy-start | bytes 196
  166.1 33.5 %all-to-all-start.2 = ((f32[16,32,512]{2,1,0:T(8,128)}), f32[16,32,512]{2,1,0:T(8,128)S(1)}, u32[]{:S(2)}, u32[]{:S(2)}) async-start(f32[16,32,512]{2,1,0:T(8,128)} %broadcast_in_dim.39), calls=%async_computation.2 | async-start | bytes 2097152 | tf_op jit(solution)/shard_map/all_to_all | solution.py:21
  200.8 25.6 %all-to-all-start.3 = ((f32[16,32,512]{2,1,0:T(8,128)}), f32[16,32,512]{2,1,0:T(8,128)S(1)}, u32[]{:S(2)}, u32[]{:S(2)}) async-start(f32[16,32,512]{2,1,0:T(8,128)} %broadcast_in_dim.40), calls=%async_computation.3 | async-start | bytes 2097152 | tf_op jit(solution)/shard_map/all_to_all | solution.py:21
  229.1 1.0 copy-start.1
